TPU v7x, 32 devices: a whole 2x2x4 slice. The times are simulated.
32 devices in a mesh: gx: 4 (over x, core), gy: 4 (over z), gz: 2 (over y).
Axes of the slice: x: 2, y: 2, z: 4, core: 2. Of those that a mesh axis runs over, the one named last changes fastest.
Arguments:
- layer_input: bfloat16 [1024, 4096], P('gz', ('gx', 'gy')), may hold values from -6 to 6
- modality: int32 [1024], P('gz'), may hold values 0 or 1
- image_spans: int32 [2, 8], replicated, may hold values from 0 to 1024, as said below
- norm_gain: float32 [2, 4096], P(None, ('gx', 'gy')), may hold values from 0.1 to 1.9
- w_qkv: bfloat16 [3, 4096, 2048], P(None, 'gz', ('gx', 'gy')), as said below
- w_out: bfloat16 [2048, 4096], P(('gx', 'gy'), 'gz'), may hold values from -0.125 to 0.125
- grad_out: bfloat16 [1024, 4096], P('gz', ('gx', 'gy')), may hold values from -6 to 6
Outputs:
- attn_out: bfloat16 [1024, 4096], P('gz', ('gx', 'gy'))
- grad_in: bfloat16 [1024, 4096], P('gz', ('gx', 'gy'))
- grad_qkv: float32 [3, 4096, 2048], P(None, 'gz', ('gx', 'gy'))
- grad_wout: float32 [2048, 4096], P(('gx', 'gy'), 'gz')
- grad_gain: float32 [2, 4096], P(None, ('gx', 'gy'))
Inputs may be any that keep to these rules, and one draw needn't show every extreme that they name: `image_spans`: row 0 holds the first position of each of 8 image spans, in increasing order, and row 1 one past its last; spans are disjoint and none is empty. `w_qkv`: entries are at most 20 * 4096 ** -0.5 in magnitude.
All inputs are finite; a program needn't handle non-finite values. No bound on the sum of `modality` on one device may be relied on, other than what follows from the above.
Results may differ from a plain program's by a relative error of at most 0.035.
The roundings to bfloat16 on the way count: a program that leaves them out, or rounds other values in their place, can miss the bound.
Values may be sent and summed in bfloat16 or wider, within the bound.
A program may use at most 128 MiB of HBM per device.

v0:
```python
import math
import jax
import jax.numpy as jnp
from jax import lax
from jax.sharding import PartitionSpec as P

epsilon = 1e-05
masked_low = -1e30


def span_index(positions, image_spans):
    inside = (positions[:, None] >= image_spans[0][None, :]) & (
        positions[:, None] < image_spans[1][None, :]
    )
    labels = jnp.arange(1, image_spans.shape[1] + 1, dtype=jnp.int32)
    return jnp.sum(jnp.where(inside, labels[None, :], 0), axis=1) - 1


def visible(query_pos, query_span, key_pos, key_span):
    causal = key_pos[None, :] <= query_pos[:, None]
    same_image = (query_span[:, None] == key_span[None, :]) & (query_span[:, None] >= 0)
    return causal | same_image


def per_device(layer_input, modality, image_spans, norm_gain, w_qkv, w_out, grad_out):
    tok_rows, local_width = layer_input.shape
    full_width = local_width * lax.axis_size(("gx", "gy"))
    head_dim = w_qkv.shape[2]
    inputs_f = layer_input.astype(jnp.float32)
    squares = lax.psum(jnp.sum(inputs_f * inputs_f, axis=1), ("gx", "gy"))
    inv_rms = lax.rsqrt(squares / full_width + epsilon)
    row_gain = jnp.where(modality[:, None] == 1, norm_gain[1][None, :], norm_gain[0][None, :])
    scaled = inputs_f * inv_rms[:, None]
    normed = (scaled * row_gain).astype(jnp.bfloat16)
    w_full = lax.all_gather(w_qkv, "gz", axis=1, tiled=True)
    wo_full = lax.all_gather(w_out, "gz", axis=1, tiled=True)
    rows_block = w_full
    projected = jnp.einsum(
        "tc,mch->mth",
        lax.all_gather(normed, ("gx", "gy"), axis=1, tiled=True),
        rows_block,
        preferred_element_type=jnp.float32,
    )
    projected = projected.astype(jnp.bfloat16)
    queries = projected[0]
    keys_values = lax.all_gather(
        jnp.concatenate([projected[1], projected[2]], axis=1), "gz", axis=0, tiled=True
    )
    key_total = keys_values.shape[0]
    query_pos = lax.axis_index("gz") * tok_rows + jnp.arange(tok_rows, dtype=jnp.int32)
    query_span = span_index(query_pos, image_spans)
    key_block = 512
    block_count = key_total // key_block
    score_scale = 1.0 / math.sqrt(head_dim)
    block_ids = jnp.arange(block_count, dtype=jnp.int32)

    def block_scores(block_idx):
        first_key = block_idx * key_block
        kv_block = lax.dynamic_slice_in_dim(keys_values, first_key, key_block, 0)
        key_pos = first_key + jnp.arange(key_block, dtype=jnp.int32)
        allowed = visible(query_pos, query_span, key_pos, span_index(key_pos, image_spans))
        scores = (
            lax.dot_general(
                queries,
                kv_block[:, :head_dim],
                (((1,), (1,)), ((), ())),
                preferred_element_type=jnp.float32,
            )
            * score_scale
        )
        return (kv_block, allowed, scores)

    def gather_stats(state, block_idx):
        maxima, summed = state
        kv_block, allowed, scores = block_scores(block_idx)
        new_maxima = jnp.maximum(maxima, jnp.max(jnp.where(allowed, scores, masked_low), axis=1))
        fresh = jnp.sum(jnp.where(allowed, jnp.exp(scores - new_maxima[:, None]), 0.0), axis=1)
        return ((new_maxima, summed * jnp.exp(maxima - new_maxima) + fresh), None)

    start_state = (
        jnp.full((tok_rows,), masked_low, jnp.float32),
        jnp.zeros((tok_rows,), jnp.float32),
    )
    (maxima, summed), unused = lax.scan(gather_stats, start_state, block_ids)
    lse = maxima + jnp.log(summed)

    def block_probs(block_idx):
        kv_block, allowed, scores = block_scores(block_idx)
        return (kv_block, jnp.where(allowed, jnp.exp(scores - lse[:, None]), 0.0))

    def attend(accum, block_idx):
        kv_block, attn_p = block_probs(block_idx)
        return (
            accum
            + jnp.dot(
                attn_p.astype(jnp.bfloat16),
                kv_block[:, head_dim:],
                preferred_element_type=jnp.float32,
            ),
            None,
        )

    attended_f, unused = lax.scan(attend, jnp.zeros((tok_rows, head_dim), jnp.float32), block_ids)
    attended = attended_f.astype(jnp.bfloat16)
    all_heads = lax.all_gather(attended, ("gx", "gy"), axis=1, tiled=True)
    out_rows = lax.all_to_all(wo_full, ("gx", "gy"), split_axis=1, concat_axis=0, tiled=True)
    head_total = out_rows.shape[0] // head_dim
    per_head = jnp.einsum(
        "thd,hdc->htc",
        all_heads.reshape(tok_rows, head_total, head_dim),
        out_rows.reshape(head_total, head_dim, local_width),
        preferred_element_type=jnp.float32,
    )
    per_head = lax.optimization_barrier(per_head.astype(jnp.bfloat16)).astype(jnp.float32)
    attn_out = jnp.sum(per_head, axis=0).astype(jnp.bfloat16)
    segment = lax.all_gather(grad_out, ("gx", "gy"), axis=1, tiled=True)
    d_accum = lax.dot_general(
        segment, wo_full, (((1,), (1,)), ((), ())), preferred_element_type=jnp.float32
    )
    partial_value = lax.dot_general(
        attended, segment, (((0,), (0,)), ((), ())), preferred_element_type=jnp.float32
    )
    d_attended = d_accum.astype(jnp.bfloat16)
    row_dots = jnp.sum(d_attended.astype(jnp.float32) * attended.astype(jnp.float32), axis=1)

    def backward_block(d_query, block_idx):
        kv_block, attn_p = block_probs(block_idx)
        d_probs = lax.dot_general(
            d_attended,
            kv_block[:, head_dim:],
            (((1,), (1,)), ((), ())),
            preferred_element_type=jnp.float32,
        )
        d_scores = (attn_p * (d_probs - row_dots[:, None]) * score_scale).astype(jnp.bfloat16)
        d_query = d_query + jnp.dot(
            d_scores, kv_block[:, :head_dim], preferred_element_type=jnp.float32
        )
        d_keys = lax.dot_general(
            d_scores, queries, (((0,), (0,)), ((), ())), preferred_element_type=jnp.float32
        )
        d_values = lax.dot_general(
            attn_p.astype(jnp.bfloat16),
            d_attended,
            (((0,), (0,)), ((), ())),
            preferred_element_type=jnp.float32,
        )
        return (d_query, jnp.concatenate([d_keys, d_values], axis=1))

    d_query_f, kv_parts = lax.scan(
        backward_block, jnp.zeros((tok_rows, head_dim), jnp.float32), block_ids
    )
    kv_grad = lax.psum_scatter(
        kv_parts.reshape(key_total, 2 * head_dim).astype(jnp.bfloat16),
        "gz",
        scatter_dimension=0,
        tiled=True,
    ).astype(jnp.float32)
    grads = jnp.stack(
        [
            d_query_f.astype(jnp.bfloat16),
            kv_grad[:, :head_dim].astype(jnp.bfloat16),
            kv_grad[:, head_dim:].astype(jnp.bfloat16),
        ]
    )
    w_grad = jnp.einsum(
        "tc,mth->mch",
        lax.all_gather(normed, ("gx", "gy"), axis=1, tiled=True),
        grads,
        preferred_element_type=jnp.float32,
    )
    grad_qkv, grad_wout = (
        lax.psum_scatter(w_grad.astype(jnp.bfloat16), "gz", scatter_dimension=1, tiled=True).astype(
            jnp.float32
        ),
        lax.psum_scatter(
            partial_value.astype(jnp.bfloat16), "gz", scatter_dimension=1, tiled=True
        ).astype(jnp.float32),
    )
    rows_block = w_full
    grad_normed = (
        lax.psum_scatter(
            jnp.einsum("mch,mth->ct", rows_block, grads, preferred_element_type=jnp.float32).astype(
                jnp.bfloat16
            ),
            ("gx", "gy"),
            scatter_dimension=0,
            tiled=True,
        )
        .astype(jnp.float32)
        .T
    )
    upstream = grad_normed * row_gain
    norm_dots = lax.psum(jnp.sum(upstream * scaled, axis=1), ("gx", "gy"))
    grad_in = (inv_rms[:, None] * (upstream - scaled * (norm_dots / full_width)[:, None])).astype(
        jnp.bfloat16
    )
    onehot = (modality[:, None] == jnp.arange(2, dtype=jnp.int32)[None, :]).astype(jnp.float32)
    local_gain = jnp.dot(onehot.T, grad_normed * scaled, precision=lax.Precision.HIGHEST)
    grad_gain = lax.psum(local_gain, "gz")
    return (attn_out, grad_in, grad_qkv, grad_wout, grad_gain)


def solution(mesh):
    in_specs = (
        P("gz", ("gx", "gy")),
        P("gz"),
        P(),
        P(None, ("gx", "gy")),
        P(None, "gz", ("gx", "gy")),
        P(("gx", "gy"), "gz"),
        P("gz", ("gx", "gy")),
    )
    out_specs = (
        P("gz", ("gx", "gy")),
        P("gz", ("gx", "gy")),
        P(None, "gz", ("gx", "gy")),
        P(("gx", "gy"), "gz"),
        P(None, ("gx", "gy")),
    )
    return jax.shard_map(
        per_device, mesh=mesh, in_specs=in_specs, out_specs=out_specs, check_vma=False
    )
```

profile of v0, /device:TPU:0, one launch (start us, length us, event | category | flops | bytes accessed | tf_op | source)
XLA Modules:
  0.0 420.7 jit_solution(4267195177550142330)
XLA Ops:
  7.3 2.7 copy.44
  10.2 35.2 %psum.21 = f32[512]{0:T(512)S(1)} all-reduce(f32[512]{0:T(512)S(1)} %fusion.65), channel_id=1, replica_groups=mesh['gx'=4,'gy'=4,'gz'=2] {'gx','gy'}, use_global_device_ids=true, to_apply=%region_1.0 | all-reduce | flops 512 | bytes 4096 | tf_op jit(solution)/shard_map/psum | solution.py:30
  45.4 0.9 fusion.66
  46.4 1.0 copy.50
  47.5 0.5 all-gather.14.cloned.1.call-update
  48.3 9.5 %all-gather.8.cloned.1.call-done = bf16[3,4096,128]{1,2,0:T(8,128)(2,1)} async-done(((bf16[3,2048,128]{1,2,0:T(8,128)(2,1)}), bf16[3,4096,128]{1,2,0:T(8,128)(2,1)}) %all-gather.8.cloned.1.call-update) | async-done | bytes 3145744 | tf_op jit(solution)/shard_map/all_gather | solution.py:35
  57.8 55.2 %all-gather.6.cloned.1.call-done = bf16[512,4096]{1,0:T(8,128)(2,1)} async-done(((bf16[512,256]{1,0:T(8,128)(2,1)}), bf16[512,4096]{1,0:T(8,128)(2,1)}) %all-gather.6.cloned.1.call-update) | async-done | bytes 4194320 | tf_op jit(solution)/shard_map/all_gather | solution.py:40
  113.0 5.0 %fusion.75 = f32[512,384]{0,1:S(1)} fusion(bf16[512,4096]{1,0:T(8,128)(2,1)} %all-gather.6.cloned.1.call-done, bf16[4096,384]{0,1:T(8,128)(2,1)} %bitcast.156), kind=kOutput, calls=%fused_computation.134 | convolution fusion | flops 1610612736 | bytes 8126464
  118.1 13.9 %all_gather.21 = bf16[1024,256]{0,1:T(8,128)(2,1)S(1)} all-gather(bf16[512,256]{0,1:T(8,128)(2,1)S(1)} %pad_maximum_fusion.1), channel_id=1, replica_groups=mesh['gx'=4,'gy'=4,'gz'=2] {'gz'}, dimensions={0}, use_global_device_ids=true | all-gather | bytes 786432 | tf_op jit(solution)/shard_map/all_gather | solution.py:46
  132.4 4.8 %while.43 = (s32[]{:T(128)}, f32[512]{0:T(512)S(1)}, f32[512]{0:T(512)S(1)}, s32[2]{0:T(128)S(1)}, s32[512]{0:T(512)S(1)}, /*index=5*/s32[2,8]{1,0:T(2,128)S(1)}...) while((s32[]{:T(128)}, f32[512]{0:T(512)S(1)}, ...), condition=%wide.region_7.8_spmd.clone, body=%wide.region_3.7_spmd.clone.sunk | while | flops 70803472 | bytes 2418638 | solution.py:84
  132.4 0.6 dynamic_slice.46
  134.8 0.6 dynamic_slice.46
  137.2 0.6 log_add_fusion
  137.7 5.9 %while.44 = (s32[]{:T(128)}, f32[512,128]{1,0:T(8,128)S(1)}, s32[2]{0:T(128)S(1)}, s32[512]{0:T(512)S(1)}, s32[2,8]{1,0:T(2,128)S(1)}, /*index=5*/bf16[1024,256]...) while((s32[]{:T(128)}, f32[512,128]{1,0:T(8,128)S(1)}, ...), condition=%wide.region_10.11_spmd.clone, body=%wide.region_8.10_spmd.clone.sunk | while | flops 136467984 | bytes 945628 | solution.py:103
  137.7 0.6 dynamic_slice.47
  139.1 1.5 fusion.118
  140.7 0.6 dynamic_slice.47
  142.1 1.5 fusion.118
  143.8 47.6 %all-gather.14.cloned.1.call-done = bf16[512,4096]{1,0:T(8,128)(2,1)} async-done(((bf16[512,256]{1,0:T(8,128)(2,1)}), bf16[512,4096]{1,0:T(8,128)(2,1)}) %all-gather.14.cloned.1.call-update) | async-done | bytes 4194320 | tf_op jit(solution)/shard_map/all_gather | solution.py:116
  191.3 4.0 multiply_reduce_fusion
  196.0 9.3 %while.45 = (s32[]{:T(128)}, f32[512,128]{1,0:T(8,128)S(1)}, bf16[2,512,256]{1,2,0:T(8,128)(2,1)S(1)}, s32[2]{0:T(128)}, s32[512]{0:T(512)S(1)}, /*index=5*/s32[...) while((s32[]{:T(128)}, f32[512,128]{1,0:T(8,128)S(1)}, ...), condition=%wide.region_15.16_spmd.clone, body=%wide.region_13.15_spmd.clone.sunk | while | flops 339367424 | bytes 6974985 | solution.py:149
  196.0 1.2 dynamic_slice.48
  198.0 1.2 fusion.129
  200.6 1.2 dynamic_slice.48
  202.7 1.2 fusion.129
  205.3 1.0 copy.56
  206.4 3.9 convolution_convert_fusion.1
  210.3 0.7 all-gather.10.cloned.1.call-update
  211.1 8.2 %reduce-scatter.5.cloned.1.call-done = bf16[512,256]{1,0:T(8,128)(2,1)} async-done(((bf16[1024,256]{1,0:T(8,128)(2,1)}), bf16[512,256]{1,0:T(8,128)(2,1)}) %reduce-scatter.5.cloned.1.call-update) | async-done | bytes 262160 | tf_op jit(solution)/shard_map/reduce_scatter | solution.py:152
  219.2 1.0 slice_bitcast_fusion.7
  220.2 5.8 %fusion.52 = bf16[4096,512]{0,1:T(8,128)(2,1)} fusion(bf16[3,4096,128]{1,2,0:T(8,128)(2,1)} %all-gather.8.cloned.1.call-done, bf16[1,512,128]{2,1,0:T(8,128)(2,1)S(1)} %get-tuple-element.678, bf16[1,512,128]{2,1,0:T(8,128)(2,1)S(1)} %get-tuple-element.677, bf16[1,512,128]{2,1,0:T(8,128)(2,1)S(1)} %convert_bitcast_fusion.1), kind=kOutput, calls=%fused_computation.84 | convolution fusion | flops 1613103104 | bytes 7733248 | tf_op jit(solution)/shard_map/mch,mth->ct/dot_general | solution.py:182
  226.3 6.1 %fusion.53 = bf16[3,4096,128]{1,2,0:T(8,128)(2,1)} fusion(bf16[512,4096]{1,0:T(8,128)(2,1)} %all-gather.6.cloned.1.call-done, bf16[1,512,128]{2,1,0:T(8,128)(2,1)S(1)} %get-tuple-element.678, bf16[1,512,128]{2,1,0:T(8,128)(2,1)S(1)} %get-tuple-element.677, bf16[1,512,128]{2,1,0:T(8,128)(2,1)S(1)} %convert_bitcast_fusion.1), kind=kOutput, calls=%fused_computation.85 | convolution fusion | flops 1612578816 | bytes 7733248 | tf_op jit(solution)/shard_map/tc,mth->mch/dot_general | solution.py:165
  232.4 1.3 copy.51
  233.8 5.5 %all-to-all-start = ((bf16[128,16,256]{2,0,1:T(8,128)(2,1)}), bf16[128,16,256]{2,0,1:T(8,128)(2,1)S(1)}, u32[]{:S(2)}, u32[]{:S(2)}) async-start(bf16[128,16,256]{2,0,1:T(8,128)(2,1)} %copy.51), calls=%async_computation | async-start | bytes 2097152 | tf_op jit(solution)/shard_map/all_to_all | solution.py:106
  239.3 3.1 reduce-scatter.11.cloned.1.call-done
  242.4 2.1 convert_element_type.104
  244.5 25.8 %all-to-all-done = bf16[128,16,256]{2,0,1:T(8,128)(2,1)S(1)} async-done(((bf16[128,16,256]{2,0,1:T(8,128)(2,1)}), bf16[128,16,256]{2,0,1:T(8,128)(2,1)S(1)}, u32[]{:S(2)}, u32[]{:S(2)}) %all-to-all-start) | async-done | bytes 1048608 | tf_op jit(solution)/shard_map/all_to_all | solution.py:106
  270.3 19.1 %all-gather.10.cloned.1.call-done = bf16[512,2048]{0,1:T(8,128)(2,1)} async-done(((bf16[512,128]{0,1:T(8,128)(2,1)}), bf16[512,2048]{0,1:T(8,128)(2,1)}) %all-gather.10.cloned.1.call-update) | async-done | bytes 2097168 | tf_op jit(solution)/shard_map/all_gather | solution.py:105
  289.4 4.8 %convolution_convert_fusion.2 = bf16[16,512,256]{2,1,0:T(8,128)(2,1)} fusion(bf16[512,16,128]{0,2,1:T(8,128)(2,1)} %bitcast.147, bf16[128,16,256]{2,0,1:T(8,128)(2,1)S(1)} %all-to-all-done), kind=kOutput, calls=%fused_computation.88 | convolution fusion | flops 538968064 | bytes 7340032 | tf_op jit(solution)/shard_map/thd,hdc->htc/dot_general | solution.py:108
  294.2 3.5 reduce_sum.98
  297.8 67.0 %reduce-scatter.7.cloned.1.call-done = bf16[256,512]{0,1:T(8,128)(2,1)} async-done(((bf16[4096,512]{0,1:T(8,128)(2,1)}), bf16[256,512]{0,1:T(8,128)(2,1)}) %reduce-scatter.7.cloned.1.call-update) | async-done | bytes 262160 | tf_op jit(solution)/shard_map/reduce_scatter | solution.py:181
  364.8 1.3 fusion.59
  366.1 30.5 %psum.22 = f32[512]{0:T(512)S(1)} all-reduce(f32[512]{0:T(512)S(1)} %fusion.59), channel_id=1, replica_groups=mesh['gx'=4,'gy'=4,'gz'=2] {'gx','gy'}, use_global_device_ids=true, to_apply=%region_19.20 | all-reduce | flops 512 | bytes 4096 | tf_op jit(solution)/shard_map/psum | solution.py:193
  396.6 1.5 fusion.63
  398.1 5.7 %psum.23 = f32[2,256]{1,0:T(2,128)} all-reduce(f32[2,256]{1,0:T(2,128)S(1)} %fusion.63), channel_id=1, replica_groups=mesh['gx'=4,'gy'=4,'gz'=2] {'gz'}, use_global_device_ids=true, to_apply=%region_22.23 | all-reduce | flops 512 | bytes 4096 | tf_op jit(solution)/shard_map/psum | solution.py:199
  403.8 6.4 %reduce-scatter.9.cloned.1.call-done = bf16[3,2048,128]{1,2,0:T(8,128)(2,1)} async-done(((bf16[3,4096,128]{1,2,0:T(8,128)(2,1)}), bf16[3,2048,128]{1,2,0:T(8,128)(2,1)}) %reduce-scatter.9.cloned.1.call-update) | async-done | bytes 1572880 | tf_op jit(solution)/shard_map/reduce_scatter | solution.py:172
  410.2 3.1 copy.59
  413.2 1.0 fusion.62
  (129 shorter events, 7.5 us)
Async XLA Ops:
  7.2 2.8 copy-start
  7.2 38.2 %copy-start.12 = (s32[512]{0:T(512)S(1)}, s32[512]{0:T(512)}, u32[]{:S(2)}) copy-start(s32[512]{0:T(512)} %param.14) | copy-start | bytes 6148
  7.2 38.2 %copy-start.14 = (f32[2,256]{1,0:T(2,128)S(1)}, f32[2,256]{1,0:T(2,128)}, u32[]{:S(2)}) copy-start(f32[2,256]{1,0:T(2,128)} %param.16) | copy-start | bytes 6148
  7.2 39.2 %copy-start.4 = (bf16[128,2048]{1,0:T(8,128)(2,1)S(1)}, bf16[128,2048]{1,0:T(8,128)(2,1)}, u32[]{:S(2)}) copy-start(bf16[128,2048]{1,0:T(8,128)(2,1)} %param.18) | copy-start | bytes 1572868
  7.2 41.0 %copy-start.5 = (s32[2,8]{1,0:T(2,128)S(1)}, s32[2,8]{1,0:T(2,128)}, u32[]{:S(2)}) copy-start(s32[2,8]{1,0:T(2,128)} %param.15) | copy-start | bytes 196
  7.2 50.6 %all-gather.8.cloned.1.call-start = ((), (), s32[]{:S(2)}) async-start(), calls=%async_computation.6 | async-start | bytes 4718592 | tf_op jit(solution)/shard_map/all_gather | solution.py:35
  10.0 103.0 %all-gather.6.cloned.1.call-start = ((), (), s32[]{:S(2)}) async-start(), calls=%async_computation.5 | async-start | bytes 4456448 | tf_op jit(solution)/shard_map/all_gather | solution.py:40
  45.4 2.8 copy-start.10
  45.4 2.7 copy-start.8
  45.4 72.6 %copy-start.6 = (f32[1,256]{1,0:T(1,128)}, f32[1,256]{1,0:T(1,128)S(1)}, u32[]{:S(2)}) copy-start(f32[1,256]{1,0:T(1,128)S(1)} %get-tuple-element.679) | copy-start | bytes 3076
  46.3 97.4 %all-gather.12.cloned.1.call-start = ((), (), s32[]{:S(2)}) async-start(), calls=%async_computation.8 | async-start | bytes 1572864 | tf_op jit(solution)/shard_map/all_gather | solution.py:36
  47.4 143.9 %all-gather.14.cloned.1.call-start = ((), (), s32[]{:S(2)}) async-start(), calls=%async_computation.9 | async-start | bytes 4456448 | tf_op jit(solution)/shard_map/all_gather | solution.py:116
  48.0 171.2 %reduce-scatter.5.cloned.1.call-start = ((), (), s32[]{:S(2)}) async-start(), calls=%async_computation.10 | async-start | bytes 786432 | tf_op jit(solution)/shard_map/reduce_scatter | solution.py:152
  143.7 62.6 %copy-start.2 = (bf16[512,128]{0,1:T(8,128)(2,1)}, bf16[512,128]{0,1:T(8,128)(2,1)S(1)}, u32[]{:S(2)}) copy-start(bf16[512,128]{0,1:T(8,128)(2,1)S(1)} %copy.49) | copy-start | bytes 393220
  206.3 36.1 %reduce-scatter.11.cloned.1.call-start = ((), (), s32[]{:S(2)}) async-start(), calls=%async_computation.13 | async-start | bytes 1572864 | tf_op jit(solution)/shard_map/reduce_scatter | solution.py:175
  210.3 79.1 %all-gather.10.cloned.1.call-start = ((), (), s32[]{:S(2)}) async-start(), calls=%async_computation.7 | async-start | bytes 2228224 | tf_op jit(solution)/shard_map/all_gather | solution.py:105
  211.0 153.8 %reduce-scatter.7.cloned.1.call-start = ((), (), s32[]{:S(2)}) async-start(), calls=%async_computation.11 | async-start | bytes 4456448 | tf_op jit(solution)/shard_map/reduce_scatter | solution.py:181
  226.1 6.4 %copy-start.1 = (bf16[128,4096]{0,1:T(8,128)(2,1)S(1)}, bf16[128,4096]{0,1:T(8,128)(2,1)}, u32[]{:S(2)}) copy-start(bf16[128,4096]{0,1:T(8,128)(2,1)} %all-gather.12.cloned.1.call-done) | copy-start | bytes 3145732
  226.1 184.1 %reduce-scatter.9.cloned.1.call-start = ((), (), s32[]{:S(2)}) async-start(), calls=%async_computation.12 | async-start | bytes 4718592 | tf_op jit(solution)/shard_map/reduce_scatter | solution.py:172
  233.8 36.5 %all-to-all-start = ((bf16[128,16,256]{2,0,1:T(8,128)(2,1)}), bf16[128,16,256]{2,0,1:T(8,128)(2,1)S(1)}, u32[]{:S(2)}, u32[]{:S(2)}) async-start(bf16[128,16,256]{2,0,1:T(8,128)(2,1)} %copy.51), calls=%async_computation | async-start | bytes 2097152 | tf_op jit(solution)/shard_map/all_to_all | solution.py:106
  289.4 75.4 %copy-start.7 = (f32[1,256]{1,0:T(1,128)S(1)}, f32[1,256]{1,0:T(1,128)}, u32[]{:S(2)}) copy-start(f32[1,256]{1,0:T(1,128)} %copy-done.6) | copy-start | bytes 3076
  289.4 75.4 %copy-start.9 = (f32[1,256]{1,0:T(1,128)S(1)}, f32[1,256]{1,0:T(1,128)}, u32[]{:S(2)}) copy-start(f32[1,256]{1,0:T(1,128)} %copy-done.8) | copy-start | bytes 3076
  289.4 75.4 %copy-start.11 = (pred[512]{0:T(512)(128)(4,1)S(1)}, pred[512]{0:T(512)(128)(4,1)}, u32[]{:S(2)}) copy-start(pred[512]{0:T(512)(128)(4,1)} %copy-done.10) | copy-start | bytes 1540
  294.2 102.4 %copy-start.13 = (s32[512]{0:T(512)S(1)}, s32[512]{0:T(512)}, u32[]{:S(2)}) copy-start(s32[512]{0:T(512)} %param.14) | copy-start | bytes 6148
  364.8 48.5 %copy-start.3 = (bf16[256,512]{0,1:T(8,128)(2,1)S(1)}, bf16[256,512]{0,1:T(8,128)(2,1)}, u32[]{:S(2)}) copy-start(bf16[256,512]{0,1:T(8,128)(2,1)} %reduce-scatter.7.cloned.1.call-done) | copy-start | bytes 786436
Sparse Core Ops, SparseCore 0:
  10.1 47.6 all-gather.7
  60.5 52.4 all-gather.5
  115.1 23.5 all-gather.11
  140.6 50.6 all-gather.13
  206.4 12.7 reduce-scatter.4
  221.9 20.3 reduce-scatter.10
  245.1 44.2 all-gather.9
  293.3 71.4 reduce-scatter.6
  367.6 42.5 reduce-scatter.8
where the time goes:
time: 421 us
  waiting for transfers between devices  243 us (58%)
  blocking collectives  85.3 us (20%)
  matrix products  40.2 us (10%)
  local copies, waits for them, and re-layouts  16.1 us (4%)
  between operations  14.2 us (3%)
  other arithmetic  11.5 us (3%)
  starting transfers between devices  6.02 us (1%)
  loops' own time  4.31 us (1%)
    reduce_scatter x1, waiting for transfers between devices, per_device(): lax.psum_scatter(jnp.einsum('mch,mth->ct', rows_block, grads, preferred_e...  67 us
    all_gather x1, waiting for transfers between devices, per_device(): lax.all_gather(normed, ('gx', 'gy'), axis=1, tiled=True)  55.2 us
    all_gather x1, waiting for transfers between devices, per_device(): segment = lax.all_gather(grad_out, ('gx', 'gy'), axis=1, tiled=True)  47.6 us
    psum x1, blocking collectives, per_device(): squares = lax.psum(jnp.sum(inputs_f * inputs_f, axis=1), ('gx', 'gy'))  35.2 us
    psum x1, blocking collectives, per_device(): norm_dots = lax.psum(jnp.sum(upstream * scaled, axis=1), ('gx', 'gy'))  30.5 us
    all_to_all x1, waiting for transfers between devices, per_device(): lax.all_to_all(wo_full, ('gx', 'gy'), split_axis=1, concat_axis=0, tiled=...  25.8 us
    all_gather x1, waiting for transfers between devices, per_device(): all_heads = lax.all_gather(attended, ('gx', 'gy'), axis=1, tiled=True)  19.1 us
    all_gather x1, blocking collectives, per_device(): lax.all_gather(jnp.concatenate([projected[1], projected[2]], axis=1), 'gz...  13.9 us
  transfers between devices with their start and end apart: 10, of which 9 were waited for; matrix products, arithmetic and copies ran while one was open for 11% of the time, Pallas kernels for 0%

commit v1 on v0

--- a/solution.py
+++ b/solution.py
@@ -113,7 +113,7 @@
     )
     per_head = lax.optimization_barrier(per_head.astype(jnp.bfloat16)).astype(jnp.float32)
     attn_out = jnp.sum(per_head, axis=0).astype(jnp.bfloat16)
-    segment = lax.all_gather(grad_out, ("gx", "gy"), axis=1, tiled=True)
+    segment = jnp.concatenate(lax.all_gather(grad_out, ("gx", "gy")), axis=1)
     d_accum = lax.dot_general(
         segment, wo_full, (((1,), (1,)), ((), ())), preferred_element_type=jnp.float32
     )

time: 421 us -> 413 us (0.981)
  waiting for transfers between devices: 243 us -> 237 us
  blocking collectives: 85.3 us -> 80.5 us
  local copies, waits for them, and re-layouts: 16.1 us -> 20.7 us
    all_gather x1, waiting for transfers between devices: 47.6 us -> 26.9 us  [per_device(): segment = jnp.concatenate(lax.all_gather(grad_out, ('gx', 'gy')), axis=1)]
    all_gather x1, waiting for transfers between devices: 0.02 us -> 15.3 us  [per_device(): wo_full = lax.all_gather(w_out, 'gz', axis=1, tiled=True)]
    reshape x0 -> x1, local copies, waits for them, and re-layouts: none -> 6.43 us  [per_device(): segment = jnp.concatenate(lax.all_gather(grad_out, ('gx', 'gy')), axis=1)]
    all_gather x1, blocking collectives: 13.9 us -> 9.12 us  [per_device(): lax.all_gather(jnp.concatenate([projected[1], projected[2]], axis=1), 'gz...]
  transfers between devices with their start and end apart: 10 -> 10, of which waited for: 9 -> 10; matrix products, arithmetic and copies ran while one was open for 11% -> 13% of each run, Pallas kernels for 0% -> 0%
where the time goes in v1:
time: 413 us; the launch traced here: 412 us
  waiting for transfers between devices  237 us (57%)
  blocking collectives  80.5 us (19%)
  matrix products  37.4 us (9%)
  local copies, waits for them, and re-layouts  20.7 us (5%)
  between operations  14.2 us (3%)
  other arithmetic  11.8 us (3%)
  starting transfers between devices  6.03 us (1%)
  loops' own time  4.36 us (1%)
    reduce_scatter x1, waiting for transfers between devices, per_device(): lax.psum_scatter(jnp.einsum('mch,mth->ct', rows_block, grads, preferred_e...  67 us
    all_gather x1, waiting for transfers between devices, per_device(): lax.all_gather(normed, ('gx', 'gy'), axis=1, tiled=True)  55.2 us
    psum x1, blocking collectives, per_device(): squares = lax.psum(jnp.sum(inputs_f * inputs_f, axis=1), ('gx', 'gy'))  35.2 us
    psum x1, blocking collectives, per_device(): norm_dots = lax.psum(jnp.sum(upstream * scaled, axis=1), ('gx', 'gy'))  30.5 us
    all_gather x1, waiting for transfers between devices, per_device(): segment = jnp.concatenate(lax.all_gather(grad_out, ('gx', 'gy')), axis=1)  26.9 us
    all_to_all x1, waiting for transfers between devices, per_device(): lax.all_to_all(wo_full, ('gx', 'gy'), split_axis=1, concat_axis=0, tiled=...  25.8 us
    all_gather x1, waiting for transfers between devices, per_device(): all_heads = lax.all_gather(attended, ('gx', 'gy'), axis=1, tiled=True)  19.1 us
    all_gather x1, waiting for transfers between devices, per_device(): wo_full = lax.all_gather(w_out, 'gz', axis=1, tiled=True)  15.3 us
  transfers between devices with their start and end apart: 10, of which 10 were waited for; matrix products, arithmetic and copies ran while one was open for 13% of the time, Pallas kernels for 0%

profile of v1, /device:TPU:0, one launch (start us, length us, event | category | flops | bytes accessed | tf_op | source)
XLA Modules:
  0.0 412.0 jit_solution(1653169652756862813)
XLA Ops:
  7.3 2.7 copy.62
  10.2 35.2 %psum.21 = f32[512]{0:T(512)S(1)} all-reduce(f32[512]{0:T(512)S(1)} %fusion.65), channel_id=1, replica_groups=mesh['gx'=4,'gy'=4,'gz'=2] {'gx','gy'}, use_global_device_ids=true, to_apply=%region_1.0 | all-reduce | flops 512 | bytes 4096 | tf_op jit(solution)/shard_map/psum | solution.py:30
  45.4 0.9 fusion.66
  46.4 0.7 all-gather.15.cloned.1.call-update
  47.1 1.0 copy.68
  48.4 9.4 %all-gather.9.cloned.1.call-done = bf16[3,4096,128]{1,2,0:T(8,128)(2,1)} async-done(((bf16[3,2048,128]{1,2,0:T(8,128)(2,1)}), bf16[3,4096,128]{1,2,0:T(8,128)(2,1)}) %all-gather.9.cloned.1.call-update) | async-done | bytes 3145744 | tf_op jit(solution)/shard_map/all_gather | solution.py:35
  57.8 55.2 %all-gather.7.cloned.1.call-done = bf16[512,4096]{1,0:T(8,128)(2,1)} async-done(((bf16[512,256]{1,0:T(8,128)(2,1)}), bf16[512,4096]{1,0:T(8,128)(2,1)}) %all-gather.7.cloned.1.call-update) | async-done | bytes 4194320 | tf_op jit(solution)/shard_map/all_gather | solution.py:40
  113.0 5.0 %fusion.75 = f32[512,384]{0,1:S(1)} fusion(bf16[512,4096]{1,0:T(8,128)(2,1)} %all-gather.7.cloned.1.call-done, bf16[4096,384]{0,1:T(8,128)(2,1)} %bitcast.163), kind=kOutput, calls=%fused_computation.134 | convolution fusion | flops 1610612736 | bytes 8126464
  118.2 9.1 %all_gather.24 = bf16[1024,256]{0,1:T(8,128)(2,1)S(1)} all-gather(bf16[512,256]{0,1:T(8,128)(2,1)S(1)} %pad_maximum_fusion.1), channel_id=1, replica_groups=mesh['gx'=4,'gy'=4,'gz'=2] {'gz'}, dimensions={0}, use_global_device_ids=true | all-gather | bytes 786432 | tf_op jit(solution)/shard_map/all_gather | solution.py:46
  127.5 4.8 %while.43 = (s32[]{:T(128)}, f32[512]{0:T(512)S(1)}, f32[512]{0:T(512)S(1)}, s32[2]{0:T(128)S(1)}, s32[512]{0:T(512)S(1)}, /*index=5*/s32[2,8]{1,0:T(2,128)S(1)}...) while((s32[]{:T(128)}, f32[512]{0:T(512)S(1)}, ...), condition=%wide.region_7.8_spmd.clone, body=%wide.region_3.7_spmd.clone.sunk | while | flops 70803472 | bytes 2418646 | solution.py:84
  127.6 0.6 dynamic_slice.46
  130.0 0.6 dynamic_slice.46
  132.4 4.5 %while.44 = (s32[]{:T(128)}, f32[512,128]{1,0:T(8,128)S(1)}, s32[2]{0:T(128)S(1)}, s32[512]{0:T(512)S(1)}, s32[2,8]{1,0:T(2,128)S(1)}, /*index=5*/bf16[1024,256]...) while((s32[]{:T(128)}, f32[512,128]{1,0:T(8,128)S(1)}, ...), condition=%wide.region_10.11_spmd.clone, body=%wide.region_8.10_spmd.clone.sunk | while | flops 136467984 | bytes 945636 | solution.py:103
  132.4 0.6 dynamic_slice.47
  133.8 0.9 fusion.118
  134.7 0.6 dynamic_slice.47
  136.0 0.8 fusion.118
  136.9 26.9 %all-gather.15.cloned.1.call-done = bf16[8192,256]{1,0:T(8,128)(2,1)} async-done(((bf16[512,256]{1,0:T(8,128)(2,1)}), bf16[8192,256]{1,0:T(8,128)(2,1)}) %all-gather.15.cloned.1.call-update) | async-done | bytes 4194320 | tf_op jit(solution)/shard_map/all_gather | solution.py:116
  163.8 6.4 %copy.71 = bf16[512,16,256]{0,2,1:T(8,128)(2,1)} copy(bf16[512,16,256]{2,0,1:T(8,128)(2,1)} %bitcast.152) | data formatting | bytes 8388608 | tf_op jit(solution)/shard_map/reshape | solution.py:116
  170.4 15.3 %all-gather.13.cloned.1.call-done = bf16[128,4096]{0,1:T(8,128)(2,1)} async-done(((bf16[128,2048]{0,1:T(8,128)(2,1)}), bf16[128,4096]{0,1:T(8,128)(2,1)}) %all-gather.13.cloned.1.call-update) | async-done | bytes 1048592 | tf_op jit(solution)/shard_map/all_gather | solution.py:36
  185.6 3.3 multiply_reduce_fusion
  189.1 6.6 %while.45 = (s32[]{:T(128)}, f32[512,128]{1,0:T(8,128)S(1)}, bf16[2,512,256]{1,2,0:T(8,128)(2,1)S(1)}, s32[2]{0:T(128)S(1)}, s32[512]{0:T(512)S(1)}, /*index=5*/...) while((s32[]{:T(128)}, f32[512,128]{1,0:T(8,128)S(1)}, ...), condition=%wide.region_15.16_spmd.clone, body=%wide.region_13.15_spmd.clone.sunk | while | flops 339367424 | bytes 6974993 | solution.py:149
  189.1 0.6 dynamic_slice.48
  192.4 0.6 dynamic_slice.48
  193.8 0.5 fusion.129
  195.7 1.0 copy.75
  196.8 4.6 %convolution_convert_fusion.1 = bf16[128,4096]{1,0:T(8,128)(2,1)} fusion(bf16[512,128]{0,1:T(8,128)(2,1)S(1)} %copy.67, bf16[512,4096]{0,1:T(8,128)(2,1)} %bitcast.151), kind=kOutput, calls=%fused_computation.86 | convolution fusion | flops 537395200 | bytes 5373952 | tf_op jit(solution)/shard_map/dot_general | solution.py:120
  201.5 0.7 all-gather.11.cloned.1.call-update
  202.3 9.2 %reduce-scatter.5.cloned.1.call-done = bf16[512,256]{1,0:T(8,128)(2,1)} async-done(((bf16[1024,256]{1,0:T(8,128)(2,1)}), bf16[512,256]{1,0:T(8,128)(2,1)}) %reduce-scatter.5.cloned.1.call-update) | async-done | bytes 262160 | tf_op jit(solution)/shard_map/reduce_scatter | solution.py:152
  211.5 1.0 slice_bitcast_fusion.7
  212.5 5.8 %fusion.52 = bf16[4096,512]{0,1:T(8,128)(2,1)} fusion(bf16[3,4096,128]{1,2,0:T(8,128)(2,1)} %all-gather.9.cloned.1.call-done, bf16[1,512,128]{2,1,0:T(8,128)(2,1)S(1)} %get-tuple-element.713, bf16[1,512,128]{2,1,0:T(8,128)(2,1)S(1)} %get-tuple-element.712, bf16[1,512,128]{2,1,0:T(8,128)(2,1)S(1)} %convert_bitcast_fusion.1), kind=kOutput, calls=%fused_computation.84 | convolution fusion | flops 1613103104 | bytes 7733248 | tf_op jit(solution)/shard_map/mch,mth->ct/dot_general | solution.py:182
  218.5 6.1 %fusion.53 = bf16[3,4096,128]{1,2,0:T(8,128)(2,1)} fusion(bf16[512,4096]{1,0:T(8,128)(2,1)} %all-gather.7.cloned.1.call-done, bf16[1,512,128]{2,1,0:T(8,128)(2,1)S(1)} %get-tuple-element.713, bf16[1,512,128]{2,1,0:T(8,128)(2,1)S(1)} %get-tuple-element.712, bf16[1,512,128]{2,1,0:T(8,128)(2,1)S(1)} %convert_bitcast_fusion.1), kind=kOutput, calls=%fused_computation.85 | convolution fusion | flops 1612578816 | bytes 7733248 | tf_op jit(solution)/shard_map/tc,mth->mch/dot_general | solution.py:165
  224.7 1.3 copy.69
  226.0 5.5 %all-to-all-start = ((bf16[128,16,256]{2,0,1:T(8,128)(2,1)}), bf16[128,16,256]{2,0,1:T(8,128)(2,1)S(1)}, u32[]{:S(2)}, u32[]{:S(2)}) async-start(bf16[128,16,256]{2,0,1:T(8,128)(2,1)} %copy.69), calls=%async_computation | async-start | bytes 2097152 | tf_op jit(solution)/shard_map/all_to_all | solution.py:106
  231.5 3.1 reduce-scatter.11.cloned.1.call-done
  234.6 2.1 convert_element_type.104
  236.7 25.8 %all-to-all-done = bf16[128,16,256]{2,0,1:T(8,128)(2,1)S(1)} async-done(((bf16[128,16,256]{2,0,1:T(8,128)(2,1)}), bf16[128,16,256]{2,0,1:T(8,128)(2,1)S(1)}, u32[]{:S(2)}, u32[]{:S(2)}) %all-to-all-start) | async-done | bytes 1048608 | tf_op jit(solution)/shard_map/all_to_all | solution.py:106
  262.5 19.1 %all-gather.11.cloned.1.call-done = bf16[512,2048]{0,1:T(8,128)(2,1)} async-done(((bf16[512,128]{0,1:T(8,128)(2,1)}), bf16[512,2048]{0,1:T(8,128)(2,1)}) %all-gather.11.cloned.1.call-update) | async-done | bytes 2097168 | tf_op jit(solution)/shard_map/all_gather | solution.py:105
  281.6 4.8 %convolution_convert_fusion.2 = bf16[16,512,256]{2,1,0:T(8,128)(2,1)} fusion(bf16[512,16,128]{0,2,1:T(8,128)(2,1)} %bitcast.153, bf16[128,16,256]{2,0,1:T(8,128)(2,1)S(1)} %all-to-all-done), kind=kOutput, calls=%fused_computation.88 | convolution fusion | flops 538968064 | bytes 7340032 | tf_op jit(solution)/shard_map/thd,hdc->htc/dot_general | solution.py:108
  286.4 3.5 reduce_sum.98
  290.0 67.0 %reduce-scatter.7.cloned.1.call-done = bf16[256,512]{0,1:T(8,128)(2,1)} async-done(((bf16[4096,512]{0,1:T(8,128)(2,1)}), bf16[256,512]{0,1:T(8,128)(2,1)}) %reduce-scatter.7.cloned.1.call-update) | async-done | bytes 262160 | tf_op jit(solution)/shard_map/reduce_scatter | solution.py:181
  357.0 1.2 fusion.59
  358.2 30.5 %psum.22 = f32[512]{0:T(512)S(1)} all-reduce(f32[512]{0:T(512)S(1)} %fusion.59), channel_id=1, replica_groups=mesh['gx'=4,'gy'=4,'gz'=2] {'gx','gy'}, use_global_device_ids=true, to_apply=%region_19.20 | all-reduce | flops 512 | bytes 4096 | tf_op jit(solution)/shard_map/psum | solution.py:193
  388.8 1.5 fusion.63
  390.2 5.7 %psum.23 = f32[2,256]{1,0:T(2,128)} all-reduce(f32[2,256]{1,0:T(2,128)S(1)} %fusion.63), channel_id=1, replica_groups=mesh['gx'=4,'gy'=4,'gz'=2] {'gz'}, use_global_device_ids=true, to_apply=%region_22.23 | all-reduce | flops 512 | bytes 4096 | tf_op jit(solution)/shard_map/psum | solution.py:199
  395.9 1.9 fusion.62
  397.9 4.5 %reduce-scatter.9.cloned.1.call-done = bf16[3,2048,128]{1,2,0:T(8,128)(2,1)} async-done(((bf16[3,4096,128]{1,2,0:T(8,128)(2,1)}), bf16[3,2048,128]{1,2,0:T(8,128)(2,1)}) %reduce-scatter.9.cloned.1.call-update) | async-done | bytes 1572880 | tf_op jit(solution)/shard_map/reduce_scatter | solution.py:172
  402.4 3.1 copy.78
  (114 shorter events, 7.4 us)
Async XLA Ops:
  7.2 2.8 copy-start
  7.2 38.2 %copy-start.5 = (s32[512]{0:T(512)S(1)}, s32[512]{0:T(512)}, u32[]{:S(2)}) copy-start(s32[512]{0:T(512)} %param.14) | copy-start | bytes 6148
  7.2 38.2 %copy-start.6 = (f32[2,256]{1,0:T(2,128)S(1)}, f32[2,256]{1,0:T(2,128)}, u32[]{:S(2)}) copy-start(f32[2,256]{1,0:T(2,128)} %param.16) | copy-start | bytes 6148
  7.2 39.9 %copy-start.3 = (bf16[128,2048]{1,0:T(8,128)(2,1)S(1)}, bf16[128,2048]{1,0:T(8,128)(2,1)}, u32[]{:S(2)}) copy-start(bf16[128,2048]{1,0:T(8,128)(2,1)} %param.18) | copy-start | bytes 1572868
  7.2 41.0 %copy-start.4 = (s32[2,8]{1,0:T(2,128)S(1)}, s32[2,8]{1,0:T(2,128)}, u32[]{:S(2)}) copy-start(s32[2,8]{1,0:T(2,128)} %param.15) | copy-start | bytes 196
  7.2 50.6 %all-gather.9.cloned.1.call-start = ((), (), s32[]{:S(2)}) async-start(), calls=%async_computation.6 | async-start | bytes 4718592 | tf_op jit(solution)/shard_map/all_gather | solution.py:35
  10.0 103.0 %all-gather.7.cloned.1.call-start = ((), (), s32[]{:S(2)}) async-start(), calls=%async_computation.5 | async-start | bytes 4456448 | tf_op jit(solution)/shard_map/all_gather | solution.py:40
  46.3 117.5 %all-gather.15.cloned.1.call-start = ((), (), s32[]{:S(2)}) async-start(), calls=%async_computation.13 | async-start | bytes 4456448 | tf_op jit(solution)/shard_map/all_gather | solution.py:116
  47.1 138.6 %all-gather.13.cloned.1.call-start = ((), (), s32[]{:S(2)}) async-start(), calls=%async_computation.8 | async-start | bytes 1572864 | tf_op jit(solution)/shard_map/all_gather | solution.py:36
  48.1 163.4 %reduce-scatter.5.cloned.1.call-start = ((), (), s32[]{:S(2)}) async-start(), calls=%async_computation.9 | async-start | bytes 786432 | tf_op jit(solution)/shard_map/reduce_scatter | solution.py:152
  170.3 26.4 %copy-start.1 = (bf16[512,128]{0,1:T(8,128)(2,1)}, bf16[512,128]{0,1:T(8,128)(2,1)S(1)}, u32[]{:S(2)}) copy-start(bf16[512,128]{0,1:T(8,128)(2,1)S(1)} %copy.67) | copy-start | bytes 393220
  196.7 37.9 %reduce-scatter.11.cloned.1.call-start = ((), (), s32[]{:S(2)}) async-start(), calls=%async_computation.12 | async-start | bytes 1572864 | tf_op jit(solution)/shard_map/reduce_scatter | solution.py:175
  201.4 80.2 %all-gather.11.cloned.1.call-start = ((), (), s32[]{:S(2)}) async-start(), calls=%async_computation.7 | async-start | bytes 2228224 | tf_op jit(solution)/shard_map/all_gather | solution.py:105
  202.2 154.8 %reduce-scatter.7.cloned.1.call-start = ((), (), s32[]{:S(2)}) async-start(), calls=%async_computation.10 | async-start | bytes 4456448 | tf_op jit(solution)/shard_map/reduce_scatter | solution.py:181
  218.3 6.4 %copy-start.2 = (bf16[128,4096]{0,1:T(8,128)(2,1)S(1)}, bf16[128,4096]{0,1:T(8,128)(2,1)}, u32[]{:S(2)}) copy-start(bf16[128,4096]{0,1:T(8,128)(2,1)} %all-gather.13.cloned.1.call-done) | copy-start | bytes 3145732
  218.3 184.1 %reduce-scatter.9.cloned.1.call-start = ((), (), s32[]{:S(2)}) async-start(), calls=%async_computation.11 | async-start | bytes 4718592 | tf_op jit(solution)/shard_map/reduce_scatter | solution.py:172
  226.0 36.5 %all-to-all-start = ((bf16[128,16,256]{2,0,1:T(8,128)(2,1)}), bf16[128,16,256]{2,0,1:T(8,128)(2,1)S(1)}, u32[]{:S(2)}, u32[]{:S(2)}) async-start(bf16[128,16,256]{2,0,1:T(8,128)(2,1)} %copy.69), calls=%async_computation | async-start | bytes 2097152 | tf_op jit(solution)/shard_map/all_to_all | solution.py:106
Sparse Core Ops, SparseCore 0:
  10.1 47.6 all-gather.8
  60.5 52.4 all-gather.6
  115.2 48.5 all-gather.14
  165.8 19.8 all-gather.12
  196.8 14.6 reduce-scatter.4
  214.2 20.3 reduce-scatter.10
  237.4 44.1 all-gather.10
  285.5 71.4 reduce-scatter.6
  359.8 42.5 reduce-scatter.8
